TPU v7x, 32 devices: a whole 2x2x4 slice. The times are simulated.
32 devices in a mesh: pole: 2 (over y), prow: 4 (over z), pcol: 4 (over x, core).
Axes of the slice: x: 2, y: 2, z: 4, core: 2. Of those that a mesh axis runs over, the one named last changes fastest.
Arguments:
- ainv_anc: bfloat16 [2, 4096, 2048], P(None, ('pole', 'prow'), 'pcol'), parts along dimension 1, may hold values from -6 to 6
- panel: bfloat16 [2, 8, 1024, 256], P(None, 'pole', ('pcol', 'prow')), parts along dimension 1, may hold values from -6 to 6
- u_inv: bfloat16 [2, 8, 256, 256], P(None, 'pole'), parts along dimension 1, may hold values from -0.01171875 to 0.01171875
- k_inv: float32 [2, 8, 256, 256], P(None, ('pole', 'pcol')), parts along dimension 1, may hold values from -6 to 6
- structure: int32 [4, 4], replicated, may hold values from -1 to 7, as said below
Outputs:
- sel_inv: float32 [2, 4096, 1024], P(None, ('pole', 'prow'), 'pcol'), parts along dimension 1
- diag_inv: float32 [2, 8, 256, 256], P(None, ('pole', 'pcol')), parts along dimension 1
There are 2 independent parts, one for each index of `pole`. A program takes and returns all parts, laid end to end along the dimension named above; an argument that names none is the same for every part. Nothing has to cross between parts.
Inputs may be any that keep to these rules, and one draw needn't show every extreme that they name: `structure`: slots g * 1 to (g + 1) * 1 - 1 of row k hold distinct blocks of g * 2 to (g + 1) * 2 - 1 in rising order, followed by -1 for empty slots; each such group of each row holds at least one block, and for every g some row fills all 1 slots of group g.
All inputs are finite; a program needn't handle non-finite values.
Results may differ from a plain program's by a relative error of at most 0.005.
Values may be sent and summed in bfloat16 or wider, within the bound.
No kernel may reach another device: no remote copies, remote signals or barrier semaphores. Data moves between devices by JAX's collectives and lax.ppermute only.
A program may use at most 128 MiB of HBM per device.

v0:
```python
import jax
import jax.numpy as jnp
from jax import lax
from jax.sharding import PartitionSpec as P


def complex_quad(z_part, s_part):
    highest = lax.Precision.HIGHEST

    def single(left, right):
        return jnp.einsum("kra,rkb->kab", left, right, precision=highest)

    real = single(z_part[0], s_part[0]) - single(z_part[1], s_part[1])
    imag = single(z_part[0], s_part[1]) + single(z_part[1], s_part[0])
    return jnp.stack([real, imag])


def local(ainv_anc, panel, u_inv, k_inv, structure):
    block_width = u_inv.shape[-1]
    total_k = u_inv.shape[1]
    own_k = k_inv.shape[1]
    n_cols = lax.axis_size("pcol")
    row_here = lax.axis_index("prow")
    col_here = lax.axis_index("pcol")
    row_blocks = ainv_anc.shape[1] // block_width
    group_blocks = ainv_anc.shape[2] // block_width
    group_slots = structure.shape[1] // n_cols
    rows_all = row_blocks * block_width
    col_struct = lax.dynamic_slice_in_dim(structure, col_here * group_slots, group_slots, 1)
    slot_live = col_struct >= 0
    slot_pos = col_struct - col_here * group_blocks
    first_block = row_here * row_blocks
    target = first_block + jnp.arange(row_blocks, dtype=jnp.int32)
    rows_in = lax.all_gather(panel, "prow", axis=2, tiled=True)

    def single(left, right):
        return jnp.einsum("knb,kbc->knc", left, right, preferred_element_type=jnp.float32)

    real = single(rows_in[0], u_inv[0]) - single(rows_in[1], u_inv[1])
    imag = single(rows_in[0], u_inv[1]) + single(rows_in[1], u_inv[0])
    placed = jnp.stack([real, imag]).astype(jnp.bfloat16)
    placed = placed.reshape(2, total_k, group_slots, block_width, block_width)
    placed = jnp.where(slot_live[None, :, :, None, None], placed, jnp.zeros((), jnp.bfloat16))
    block_ids = jnp.arange(group_blocks, dtype=jnp.int32)
    pick_table = (slot_pos[:, :, None] == block_ids[None, None, :]).astype(jnp.bfloat16)
    ainv_blocks = ainv_anc.reshape(2, rows_all, group_blocks, block_width)

    def one_node(items):
        table_k, rows_k = items
        picked = jnp.einsum(
            "sg,cigw->cisw", table_k, ainv_blocks, preferred_element_type=jnp.float32
        )
        picked = picked.astype(jnp.bfloat16).reshape(2, rows_all, group_slots * block_width)
        right = rows_k.reshape(2, group_slots * block_width, block_width)
        real = jnp.dot(picked[0], right[0], preferred_element_type=jnp.float32) - jnp.dot(
            picked[1], right[1], preferred_element_type=jnp.float32
        )
        imag = jnp.dot(picked[0], right[1], preferred_element_type=jnp.float32) + jnp.dot(
            picked[1], right[0], preferred_element_type=jnp.float32
        )
        return jnp.stack([real, imag])

    per_node = lax.map(one_node, (pick_table, jnp.moveaxis(placed, 1, 0)))
    partial_value = jnp.transpose(per_node, (1, 2, 0, 3))
    row_table = (col_struct[:, None, :] == target[None, :, None]).astype(jnp.bfloat16)
    z_rows = jnp.einsum("kts,ckswb->cktwb", row_table, placed, preferred_element_type=jnp.float32)
    z_rows = z_rows.astype(jnp.bfloat16).reshape(2, total_k, rows_all, block_width)
    summed = lax.psum_scatter(
        partial_value.reshape(2, rows_all, total_k * block_width),
        "pcol",
        scatter_dimension=2,
        tiled=True,
    )
    own_struct = lax.dynamic_slice_in_dim(structure, col_here * own_k, own_k, 0)
    member = jnp.any(own_struct[:, :, None] == target[None, None, :], axis=1)
    selected = -summed.reshape(2, row_blocks, block_width, own_k, block_width)
    selected = jnp.where(member.T[None, :, None, :, None], selected, 0.0)
    sel_inv = selected.reshape(2, rows_all, own_k * block_width)
    received = lax.all_to_all(z_rows, "pcol", split_axis=1, concat_axis=1, tiled=True)
    z_own = (
        received.astype(jnp.float32).reshape(2, n_cols, own_k, rows_all, block_width).sum(axis=1)
    )
    quad_term = complex_quad(z_own, selected.reshape(2, rows_all, own_k, block_width))
    total_sum = lax.psum(quad_term, "prow")
    diag_inv = k_inv - total_sum
    return (sel_inv, diag_inv)


def solution(mesh):
    placed = (
        P(None, ("pole", "prow"), "pcol"),
        P(None, "pole", ("pcol", "prow"), None),
        P(None, "pole", None, None),
        P(None, ("pole", "pcol"), None, None),
        P(),
    )
    return jax.shard_map(
        local,
        mesh=mesh,
        in_specs=placed,
        out_specs=(P(None, ("pole", "prow"), "pcol"), P(None, ("pole", "pcol"), None, None)),
        check_vma=False,
    )
```

profile of v0, /device:TPU:0, one launch (start us, length us, event | category | flops | bytes accessed | tf_op | source)
XLA Modules:
  0.0 170.8 jit_solution(10218093751577018464)
XLA Ops:
  8.0 1.3 reshape.276
  11.2 29.1 %all-gather.2.cloned.1.call-done = bf16[2,4,256,256]{3,2,1,0:T(8,128)(2,1)} async-done(((bf16[2,4,64,256]{3,2,1,0:T(8,128)(2,1)}), bf16[2,4,256,256]{3,2,1,0:T(8,128)(2,1)}) %all-gather.2.cloned.1.call-update) | async-done | bytes 1048592 | tf_op jit(solution)/shard_map/all_gather | solution.py:34
  40.3 1.6 fusion.13
  41.9 1.3 fusion.17
  44.1 13.4 %while.10 = (s32[]{:T(128)}, f32[4,2,512,256]{3,2,1,0:T(8,128)}, bf16[4,1,2]{2,1,0:T(2,128)(2,1)S(1)}, bf16[2,512,2,256]{3,2,1,0:T(2,128)(2,1)S(1)}, bf16[4,2,1,256,256]{4,3,0,2,1:T(8,128)(2,1)S(1)}, /*index=5*/s32[]{:T(128)}) while((s32[]{:T(128)}, f32[4,2,512,256]{3,2,1,0:T(8,128)}, bf16[4,1,2]{2,1,0:T(2,128)(2,1)S(1)}, ...), condition=%wide.region_2.3_spmd, body=%wide.region_1.2_spmd.sunk | while | flops 270008320 | bytes 9962073 | solution.py:63
  44.1 1.2 fusion.42
  46.4 1.0 fusion.47
  47.4 1.2 fusion.42
  49.7 1.1 fusion.47
  50.8 1.2 fusion.42
  53.1 1.1 fusion.47
  54.2 1.2 fusion.42
  56.4 1.0 fusion.47
  57.5 4.8 %copy.21 = f32[4,2,64,8,256]{4,3,0,2,1:T(8,128)} copy(f32[4,2,64,8,256]{4,3,2,1,0:T(8,128)} %bitcast.135) | data formatting | bytes 8388608 | tf_op jit(solution)/shard_map/reshape | solution.py:69
  63.0 1.5 copy.17
  64.5 3.8 %all-to-all-start = ((bf16[2,4,512,256]{3,2,0,1:T(8,128)(2,1)}), bf16[2,4,512,256]{3,2,0,1:T(8,128)(2,1)S(1)}, u32[]{:S(2)}, u32[]{:S(2)}) async-start(bf16[2,4,512,256]{3,2,0,1:T(8,128)(2,1)} %copy.17), calls=%async_computation.1 | async-start | bytes 4194304 | tf_op jit(solution)/shard_map/all_to_all | solution.py:79
  69.2 36.9 %all-to-all-done = bf16[2,4,512,256]{3,2,0,1:T(8,128)(2,1)S(1)} async-done(((bf16[2,4,512,256]{3,2,0,1:T(8,128)(2,1)}), bf16[2,4,512,256]{3,2,0,1:T(8,128)(2,1)S(1)}, u32[]{:S(2)}, u32[]{:S(2)}) %all-to-all-start) | async-done | bytes 2097184 | tf_op jit(solution)/shard_map/all_to_all | solution.py:79
  106.4 11.5 %reduce-scatter.2.cloned.1.call-done = f32[2,512,256]{2,1,0:T(8,128)} async-done(((f32[2,512,1024]{2,1,0:T(8,128)}), f32[2,512,256]{2,1,0:T(8,128)}) %reduce-scatter.2.cloned.1.call-update) | async-done | bytes 1048592 | tf_op jit(solution)/shard_map/reduce_scatter | solution.py:68
  117.9 2.3 %fusion.26 = (f32[2,512,256]{2,1,0:T(8,128)S(1)}, f32[2,512,256]{2,1,0:T(8,128)}) fusion(f32[2,512,256]{2,1,0:T(8,128)} %reduce-scatter.2.cloned.1.call-done, pred[512]{0:T(512)(128)(4,1)S(1)} %broadcast_in_dim.53), kind=kLoop, calls=%fused_computation.59 | loop fusion | flops 524288 | bytes 3146240 | tf_op jit(solution)/shard_map/neg | solution.py:76
  120.5 1.0 fusion.19
  122.5 1.0 fusion.10
  123.5 1.0 fusion.11
  125.4 37.0 %all-reduce.2.cloned.1.call-done = f32[2,1,256,256]{3,2,1,0:T(8,128)} async-done(((f32[2,1,256,256]{3,2,1,0:T(8,128)}), f32[2,1,256,256]{3,2,1,0:T(8,128)}) %all-reduce.2.cloned.1.call-update) | async-done | bytes 524304 | tf_op jit(solution)/shard_map/psum | solution.py:84
  162.4 1.9 %sub.26 = f32[2,1,256,256]{3,2,1,0:T(8,128)} subtract(f32[2,1,256,256]{3,2,1,0:T(8,128)S(1)} %copy-done.2, f32[2,1,256,256]{3,2,1,0:T(8,128)} %all-reduce.2.cloned.1.call-done) | non-fusion elementwise | flops 131072 | bytes 1572864 | tf_op jit(solution)/shard_map/sub | solution.py:85
  (56 shorter events, 11.5 us)
Async XLA Ops:
  7.2 34.7 %copy-start = (bf16[2,4,256,256]{3,2,1,0:T(8,128)(2,1)S(1)}, bf16[2,4,256,256]{3,2,1,0:T(8,128)(2,1)}, u32[]{:S(2)}) copy-start(bf16[2,4,256,256]{3,2,1,0:T(8,128)(2,1)} %param.9) | copy-start | bytes 3145732
  7.2 33.1 %all-gather.2.cloned.1.call-start = ((), (), s32[]{:S(2)}) async-start(), calls=%async_computation.2 | async-start | bytes 1310720 | tf_op jit(solution)/shard_map/all_gather | solution.py:34
  7.9 110.0 %reduce-scatter.2.cloned.1.call-start = ((), (), s32[]{:S(2)}) async-start(), calls=%async_computation.3 | async-start | bytes 5242880 | tf_op jit(solution)/shard_map/reduce_scatter | solution.py:68
  40.3 3.0 %copy-start.1 = (bf16[2,4,256,256]{3,2,1,0:T(8,128)(2,1)S(1)}, bf16[2,4,256,256]{3,2,1,0:T(8,128)(2,1)}, u32[]{:S(2)}) copy-start(bf16[2,4,256,256]{3,2,1,0:T(8,128)(2,1)} %all-gather.2.cloned.1.call-done) | copy-start | bytes 3145732
  64.5 41.6 %all-to-all-start = ((bf16[2,4,512,256]{3,2,0,1:T(8,128)(2,1)}), bf16[2,4,512,256]{3,2,0,1:T(8,128)(2,1)S(1)}, u32[]{:S(2)}, u32[]{:S(2)}) async-start(bf16[2,4,512,256]{3,2,0,1:T(8,128)(2,1)} %copy.17), calls=%async_computation.1 | async-start | bytes 4194304 | tf_op jit(solution)/shard_map/all_to_all | solution.py:79
  68.2 94.1 %all-reduce.2.cloned.1.call-start = ((), (), s32[]{:S(2)}) async-start(), calls=%async_computation.4 | async-start | bytes 1048576 | tf_op jit(solution)/shard_map/psum | solution.py:84
  120.4 41.9 %copy-start.2 = (f32[2,1,256,256]{3,2,1,0:T(8,128)S(1)}, f32[2,1,256,256]{3,2,1,0:T(8,128)}, u32[]{:S(2)}) copy-start(f32[2,1,256,256]{3,2,1,0:T(8,128)} %param.10) | copy-start | bytes 1572868
Sparse Core Ops, SparseCore 0:
  9.6 30.6 all-gather.1
  62.4 55.4 reduce-scatter.1
  125.5 36.8 all-reduce.1
where the time goes:
time: 171 us
  waiting for transfers between devices  115 us (67%)
  matrix products  16.1 us (9%)
  between operations  13.9 us (8%)
  other arithmetic  12.6 us (7%)
  local copies, waits for them, and re-layouts  8.88 us (5%)
  starting transfers between devices  3.88 us (2%)
    psum x1, waiting for transfers between devices, local(): total_sum = lax.psum(quad_term, 'prow')  37 us
    all_to_all x1, waiting for transfers between devices, local(): lax.all_to_all(z_rows, 'pcol', split_axis=1, concat_axis=1, tiled=True)  36.9 us
    all_gather x1, waiting for transfers between devices, local(): rows_in = lax.all_gather(panel, 'prow', axis=2, tiled=True)  29.1 us
    reduce_scatter x1, waiting for transfers between devices, local(): lax.psum_scatter(partial_value.reshape(2, rows_all, total_k * block_width...  11.5 us
    dot_general x4, matrix products, one_node(): jnp.einsum('sg,cigw->cisw', table_k, ainv_blocks, preferred_element_type=...  4.94 us
    reshape x1, local copies, waits for them, and re-layouts, local(): partial_value.reshape(2, rows_all, total_k * block_width)  4.76 us
    dynamic_update_slice x4, other arithmetic, local(): per_node = lax.map(one_node, (pick_table, jnp.moveaxis(placed, 1, 0)))  4.27 us
    dot_general x4, matrix products, single(): return jnp.einsum('kra,rkb->kab', left, right, precision=highest)  4.02 us
  transfers between devices with their start and end apart: 4, of which 4 were waited for; matrix products, arithmetic and copies ran while one was open for 4% of the time, Pallas kernels for 0%

commit v1 on v0

--- a/solution.py
+++ b/solution.py
@@ -81,7 +81,7 @@
         received.astype(jnp.float32).reshape(2, n_cols, own_k, rows_all, block_width).sum(axis=1)
     )
     quad_term = complex_quad(z_own, selected.reshape(2, rows_all, own_k, block_width))
-    total_sum = lax.psum(quad_term, "prow")
+    total_sum = jnp.sum(lax.all_gather(quad_term, "prow"), axis=0)
     diag_inv = k_inv - total_sum
     return (sel_inv, diag_inv)
 

time: 171 us -> 179 us (1.047)
  waiting for transfers between devices: 115 us -> 122 us
    all_gather x0 -> x1, waiting for transfers between devices: none -> 44.1 us  [local(): total_sum = jnp.sum(lax.all_gather(quad_term, 'prow'), axis=0)]
    psum x1 -> x0, waiting for transfers between devices: 37 us -> none  [local(): total_sum = lax.psum(quad_term, 'prow')]
where the time goes in v1:
time: 179 us
  waiting for transfers between devices  122 us (68%)
  matrix products  16.1 us (9%)
  between operations  13.9 us (8%)
  other arithmetic  13.4 us (7%)
  local copies, waits for them, and re-layouts  8.88 us (5%)
  starting transfers between devices  3.88 us (2%)
    all_gather x1, waiting for transfers between devices, local(): total_sum = jnp.sum(lax.all_gather(quad_term, 'prow'), axis=0)  44.1 us
    all_to_all x1, waiting for transfers between devices, local(): lax.all_to_all(z_rows, 'pcol', split_axis=1, concat_axis=1, tiled=True)  36.9 us
    all_gather x1, waiting for transfers between devices, local(): rows_in = lax.all_gather(panel, 'prow', axis=2, tiled=True)  29.1 us
    reduce_scatter x1, waiting for transfers between devices, local(): lax.psum_scatter(partial_value.reshape(2, rows_all, total_k * block_width...  11.5 us
    dot_general x4, matrix products, one_node(): jnp.einsum('sg,cigw->cisw', table_k, ainv_blocks, preferred_element_type=...  4.94 us
    reshape x1, local copies, waits for them, and re-layouts, local(): partial_value.reshape(2, rows_all, total_k * block_width)  4.76 us
    dynamic_update_slice x4, other arithmetic, local(): per_node = lax.map(one_node, (pick_table, jnp.moveaxis(placed, 1, 0)))  4.27 us
    dot_general x4, matrix products, single(): return jnp.einsum('kra,rkb->kab', left, right, precision=highest)  4.02 us
  transfers between devices with their start and end apart: 4, of which 4 were waited for; matrix products, arithmetic and copies ran while one was open for 4% of the time, Pallas kernels for 0%

profile of v1, /device:TPU:0, one launch (start us, length us, event | category | flops | bytes accessed | tf_op | source)
XLA Modules:
  0.0 178.7 jit_solution(3301416027574723989)
XLA Ops:
  8.0 1.3 reshape.277
  11.2 29.1 %all-gather.4.cloned.1.call-done = bf16[2,4,256,256]{3,2,1,0:T(8,128)(2,1)} async-done(((bf16[2,4,64,256]{3,2,1,0:T(8,128)(2,1)}), bf16[2,4,256,256]{3,2,1,0:T(8,128)(2,1)}) %all-gather.4.cloned.1.call-update) | async-done | bytes 1048592 | tf_op jit(solution)/shard_map/all_gather | solution.py:34
  40.3 1.6 fusion.13
  41.9 1.3 fusion.17
  44.1 13.4 %while.10 = (s32[]{:T(128)}, f32[4,2,512,256]{3,2,1,0:T(8,128)}, bf16[4,1,2]{2,1,0:T(2,128)(2,1)S(1)}, bf16[2,512,2,256]{3,2,1,0:T(2,128)(2,1)S(1)}, bf16[4,2,1,256,256]{4,3,0,2,1:T(8,128)(2,1)S(1)}, /*index=5*/s32[]{:T(128)}) while((s32[]{:T(128)}, f32[4,2,512,256]{3,2,1,0:T(8,128)}, bf16[4,1,2]{2,1,0:T(2,128)(2,1)S(1)}, ...), condition=%wide.region_2.3_spmd, body=%wide.region_1.2_spmd.sunk | while | flops 270008320 | bytes 9962073 | solution.py:63
  44.1 1.2 fusion.42
  46.4 1.0 fusion.47
  47.4 1.2 fusion.42
  49.7 1.1 fusion.47
  50.8 1.2 fusion.42
  53.1 1.1 fusion.47
  54.2 1.2 fusion.42
  56.4 1.0 fusion.47
  57.5 4.8 %copy.21 = f32[4,2,64,8,256]{4,3,0,2,1:T(8,128)} copy(f32[4,2,64,8,256]{4,3,2,1,0:T(8,128)} %bitcast.140) | data formatting | bytes 8388608 | tf_op jit(solution)/shard_map/reshape | solution.py:69
  63.0 1.5 copy.17
  64.5 3.8 %all-to-all-start = ((bf16[2,4,512,256]{3,2,0,1:T(8,128)(2,1)}), bf16[2,4,512,256]{3,2,0,1:T(8,128)(2,1)S(1)}, u32[]{:S(2)}, u32[]{:S(2)}) async-start(bf16[2,4,512,256]{3,2,0,1:T(8,128)(2,1)} %copy.17), calls=%async_computation.1 | async-start | bytes 4194304 | tf_op jit(solution)/shard_map/all_to_all | solution.py:79
  69.2 36.9 %all-to-all-done = bf16[2,4,512,256]{3,2,0,1:T(8,128)(2,1)S(1)} async-done(((bf16[2,4,512,256]{3,2,0,1:T(8,128)(2,1)}), bf16[2,4,512,256]{3,2,0,1:T(8,128)(2,1)S(1)}, u32[]{:S(2)}, u32[]{:S(2)}) %all-to-all-start) | async-done | bytes 2097184 | tf_op jit(solution)/shard_map/all_to_all | solution.py:79
  106.4 11.5 %reduce-scatter.2.cloned.1.call-done = f32[2,512,256]{2,1,0:T(8,128)} async-done(((f32[2,512,1024]{2,1,0:T(8,128)}), f32[2,512,256]{2,1,0:T(8,128)}) %reduce-scatter.2.cloned.1.call-update) | async-done | bytes 1048592 | tf_op jit(solution)/shard_map/reduce_scatter | solution.py:68
  117.9 2.3 %fusion.26 = (f32[2,512,256]{2,1,0:T(8,128)S(1)}, f32[2,512,256]{2,1,0:T(8,128)}) fusion(f32[2,512,256]{2,1,0:T(8,128)} %reduce-scatter.2.cloned.1.call-done, pred[512]{0:T(512)(128)(4,1)S(1)} %broadcast_in_dim.53), kind=kLoop, calls=%fused_computation.61 | loop fusion | flops 524288 | bytes 3146240 | tf_op jit(solution)/shard_map/neg | solution.py:76
  120.4 1.0 fusion.19
  122.5 1.0 fusion.10
  123.5 1.0 fusion.11
  125.4 44.1 %all-gather.6.cloned.1.call-done = f32[8,1,256,256]{3,2,1,0:T(8,128)} async-done(((f32[2,1,256,256]{3,2,1,0:T(8,128)}), f32[8,1,256,256]{3,2,1,0:T(8,128)}) %all-gather.6.cloned.1.call-update) | async-done | bytes 2097168 | tf_op jit(solution)/shard_map/all_gather | solution.py:84
  169.5 1.8 bitcast_reduce_fusion
  (57 shorter events, 12.3 us)
Async XLA Ops:
  7.2 34.7 %copy-start = (bf16[2,4,256,256]{3,2,1,0:T(8,128)(2,1)S(1)}, bf16[2,4,256,256]{3,2,1,0:T(8,128)(2,1)}, u32[]{:S(2)}) copy-start(bf16[2,4,256,256]{3,2,1,0:T(8,128)(2,1)} %param.9) | copy-start | bytes 3145732
  7.2 33.1 %all-gather.4.cloned.1.call-start = ((), (), s32[]{:S(2)}) async-start(), calls=%async_computation.2 | async-start | bytes 1310720 | tf_op jit(solution)/shard_map/all_gather | solution.py:34
  7.9 110.0 %reduce-scatter.2.cloned.1.call-start = ((), (), s32[]{:S(2)}) async-start(), calls=%async_computation.3 | async-start | bytes 5242880 | tf_op jit(solution)/shard_map/reduce_scatter | solution.py:68
  40.3 3.0 %copy-start.1 = (bf16[2,4,256,256]{3,2,1,0:T(8,128)(2,1)S(1)}, bf16[2,4,256,256]{3,2,1,0:T(8,128)(2,1)}, u32[]{:S(2)}) copy-start(bf16[2,4,256,256]{3,2,1,0:T(8,128)(2,1)} %all-gather.4.cloned.1.call-done) | copy-start | bytes 3145732
  64.5 41.6 %all-to-all-start = ((bf16[2,4,512,256]{3,2,0,1:T(8,128)(2,1)}), bf16[2,4,512,256]{3,2,0,1:T(8,128)(2,1)S(1)}, u32[]{:S(2)}, u32[]{:S(2)}) async-start(bf16[2,4,512,256]{3,2,0,1:T(8,128)(2,1)} %copy.17), calls=%async_computation.1 | async-start | bytes 4194304 | tf_op jit(solution)/shard_map/all_to_all | solution.py:79
  68.2 101.3 %all-gather.6.cloned.1.call-start = ((), (), s32[]{:S(2)}) async-start(), calls=%async_computation.4 | async-start | bytes 2621440 | tf_op jit(solution)/shard_map/all_gather | solution.py:84
  121.5 49.8 %copy-start.2 = (f32[2,1,256,256]{3,2,1,0:T(8,128)S(1)}, f32[2,1,256,256]{3,2,1,0:T(8,128)}, u32[]{:S(2)}) copy-start(f32[2,1,256,256]{3,2,1,0:T(8,128)} %param.10) | copy-start | bytes 1572868
Sparse Core Ops, SparseCore 0:
  9.6 30.6 all-gather.3
  62.4 55.4 reduce-scatter.1
  125.5 43.9 all-gather.5
